TPU v7x, 32 devices: a whole 2x2x4 slice. The times are simulated.
32 devices in a mesh: dp: 8 (over z, x), tensor: 4 (over y, core).
Axes of the slice: x: 2, y: 2, z: 4, core: 2. Of those that a mesh axis runs over, the one named last changes fastest.
Arguments:
- logits: bfloat16 [16, 128, 19456], P('dp', None, 'tensor'), may hold values from -110 to 290
- token_ids: int32 [16, 128], P('dp'), may hold values from 0 to 19455
- response_mask: int32 [16, 128], P('dp'), may hold values 0 or 1
- lengths: int32 [16], P('dp'), may hold values from 16 to 128
- prompt_of: int32 [16], P('dp'), may hold values from 0 to 1, as said below
- old_logprob: float32 [16, 128], P('dp'), may hold values from -14 to -10
- ref_logprob: bfloat16 [16, 128], P(None, 'dp'), may hold values from -14 to -10
- advantages: float32 [16, 128], P('dp'), may hold values from -8 to 8
- returns: float32 [16, 128], P('dp'), may hold values from -6 to 6
- critic_hidden: bfloat16 [16, 128, 5120], P(None, 'dp', 'tensor'), may hold values from -6 to 6
- value_weight: bfloat16 [5120], P('tensor'), may hold values from -0.078125 to 0.078125
Outputs:
- token_loss: float32 [16, 128], P('dp')
- critic_grad: bfloat16 [16, 128, 5120], P(None, 'dp', 'tensor')
Inputs may be any that keep to these rules, and one draw needn't show every extreme that they name: `prompt_of`: each of the 2 prompts is named by exactly 8 sequences.
All inputs are finite; a program needn't handle non-finite values. No bound on the sum of `response_mask` on one device may be relied on, other than what follows from the above.
Results may differ from a plain program's by a relative error of at most 0.001.
Values may be sent and summed in bfloat16 or wider, within the bound.
No kernel may reach another device: no remote copies, remote signals or barrier semaphores. Data moves between devices by JAX's collectives and lax.ppermute only.
A program may use at most 64 MiB of HBM per device.

v0:
```python
import jax
import jax.numpy as jnp
from jax import lax
from jax.sharding import PartitionSpec as P

RESPONSES = 8


def per_device(
    logits,
    token_ids,
    response_mask,
    lengths,
    prompt_of,
    old_logprob,
    ref_logprob,
    advantages,
    returns,
    critic_hidden,
    value_weight,
):
    highest = lax.Precision.HIGHEST
    seq_rows, seq_len, vocab_width = logits.shape
    all_seqs, tile_len, feat_count = critic_hidden.shape
    dp_size = lax.axis_size("dp")
    head_weight = value_weight.astype(jnp.float32)
    tile_rows = critic_hidden.reshape(all_seqs * tile_len, feat_count)
    local_part = jnp.dot(tile_rows, value_weight, preferred_element_type=jnp.float32).reshape(
        all_seqs, tile_len
    )
    partial_value, ref_rows = (
        lax.all_to_all(local_part, "dp", split_axis=0, concat_axis=1, tiled=True),
        lax.all_to_all(
            ref_logprob.astype(jnp.float32), "dp", split_axis=0, concat_axis=1, tiled=True
        ),
    )
    position = lax.broadcasted_iota(jnp.int32, (seq_rows, seq_len), 1)
    live_mask = (response_mask * (position < lengths[:, None]).astype(jnp.int32)).astype(
        jnp.float32
    )
    prompt_count = seq_rows * dp_size // RESPONSES
    prompt_hot = (
        prompt_of[:, None] == lax.broadcasted_iota(jnp.int32, (seq_rows, prompt_count), 1)
    ).astype(jnp.float32)
    seq_tokens = jnp.sum(live_mask, axis=1)
    seq_total = jnp.sum(live_mask * advantages, axis=1)
    seq_square = jnp.sum(live_mask * advantages * advantages, axis=1)
    moments = jnp.dot(jnp.stack([seq_tokens, seq_total, seq_square]), prompt_hot, precision=highest)
    count_all, total_all, square_all = lax.psum((moments[0], moments[1], moments[2]), "dp")
    count_floor = jnp.maximum(count_all, 1.0)
    prompt_mean = total_all / count_floor
    prompt_var = (square_all - prompt_mean * total_all) / count_floor
    row_mean = jnp.dot(prompt_hot, prompt_mean, precision=highest)
    row_scale = lax.rsqrt(jnp.dot(prompt_hot, prompt_var, precision=highest) + 1.0)
    whitened = (advantages - row_mean[:, None]) * row_scale[:, None]
    local_top = jnp.max(logits, axis=2).astype(jnp.float32)
    local_sum = jnp.sum(jnp.exp(logits.astype(jnp.float32) - local_top[:, :, None]), axis=2)
    vocab_start = lax.axis_index("tensor") * vocab_width
    shifted = token_ids - vocab_start
    in_shard = (shifted >= 0) & (shifted < vocab_width)
    clipped_ids = jnp.clip(shifted, 0, vocab_width - 1)
    picked = jnp.take_along_axis(logits, clipped_ids[:, :, None], axis=2)[:, :, 0].astype(
        jnp.float32
    )
    target_part = jnp.where(in_shard, picked, 0.0)
    row_max = lax.pmax(local_top, "tensor")
    rescaled = local_sum * jnp.exp(local_top - row_max)
    total_sum, target_logit, value_pred = lax.psum((rescaled, target_part, partial_value), "tensor")
    logprob = target_logit - (row_max + jnp.log(total_sum))
    prob_ratio = jnp.exp(jnp.clip(logprob - old_logprob, -20.0, 20.0))
    surrogate = jnp.maximum(-whitened * prob_ratio, -whitened * jnp.clip(prob_ratio, 0.8, 1.2))
    surrogate = jnp.where(whitened < 0.0, jnp.minimum(surrogate, -3.0 * whitened), surrogate)
    ref_drift = jnp.clip(ref_rows - logprob, -20.0, 20.0)
    penalty = jnp.clip(jnp.exp(ref_drift) - ref_drift - 1.0, -10.0, 10.0)
    value_error = value_pred - returns
    token_loss = live_mask * (surrogate + 0.1 * penalty + 0.25 * value_error * value_error)
    grad_coeff = 32.0 * live_mask * value_error
    returned = lax.all_to_all(grad_coeff, "dp", split_axis=1, concat_axis=0, tiled=True)
    critic_grad = (returned[:, :, None] * head_weight[None, None, :]).astype(jnp.bfloat16)
    return (token_loss, critic_grad)


def solution(mesh):
    in_specs = (
        P("dp", None, "tensor"),
        P("dp", None),
        P("dp", None),
        P("dp"),
        P("dp"),
        P("dp", None),
        P(None, "dp"),
        P("dp", None),
        P("dp", None),
        P(None, "dp", "tensor"),
        P("tensor"),
    )
    out_specs = (P("dp", None), P(None, "dp", "tensor"))
    return jax.shard_map(
        per_device, mesh=mesh, in_specs=in_specs, out_specs=out_specs, check_vma=False
    )
```

profile of v0, /device:TPU:0, one launch (start us, length us, event | category | flops | bytes accessed | tf_op | source)
XLA Modules:
  0.0 71.6 jit_solution(9083070051270361440)
XLA Ops:
  0.6 0.0 copy-start
  0.6 0.0 copy-start.1
  0.7 1.4 %convert.1 = f32[8,2,16]{2,1,0:T(2,128)} convert(bf16[8,2,16]{2,1,0:T(2,128)(2,1)} %bitcast.45) | non-fusion elementwise | flops 256 | bytes 1536 | tf_op jit(solution)/shard_map/all_to_all | solution.py:33
  2.1 7.3 %all-to-all-start = ((f32[8,2,16]{2,1,0:T(2,128)}), f32[8,2,16]{2,1,0:T(2,128)S(1)}, u32[]{:S(2)}, u32[]{:S(2)}) async-start(f32[8,2,16]{2,1,0:T(2,128)} %convert.1), calls=%async_computation | async-start | bytes 16384 | tf_op jit(solution)/shard_map/all_to_all | solution.py:33
  9.4 0.0 copy-start.3
  9.4 2.1 %reduce_max.9 = bf16[2,128]{1,0:T(2,128)(2,1)S(1)} reduce(bf16[2,128,4864]{2,1,0:T(8,128)(2,1)} %param.11, bf16[]{:T(256)} %constant.27.clone.1), dimensions={2}, to_apply=%region_7.0 | reduce | flops 1244928 | bytes 2490882 | tf_op jit(solution)/shard_map/reduce_max | solution.py:56
  11.5 0.0 copy-start.6
  11.5 0.0 copy-start.8
  11.6 0.0 copy-start.4
  11.6 0.0 copy-start.9
  11.6 6.6 %pmax.7 = f32[2,128]{1,0:T(2,128)S(1)} all-reduce(bf16[2,128]{1,0:T(2,128)(2,1)S(1)} %reduce_max.9), channel_id=1, replica_groups=mesh['dp'=8,'tensor'=4] {'tensor'}, use_global_device_ids=true, to_apply=%region_8.9 | all-reduce | flops 256 | bytes 1536 | tf_op jit(solution)/shard_map/pmax | solution.py:66
  18.2 1.0 %exponential_reduce_fusion = f32[2,128]{1,0:T(2,128)S(1)} fusion(bf16[2,128,4864]{2,1,0:T(8,128)(2,1)S(1)} %copy-done.1, f32[2,128]{1,0:T(2,128)S(1)} %convert_element_type.27), kind=kLoop, calls=%fused_computation.1 | loop fusion | flops 3735296 | bytes 2492416 | tf_op jit(solution)/shard_map/reduce_sum | solution.py:57
  19.3 1.5 %fusion.2 = f32[1,8,2,16]{3,0,2,1:T(1,128)} fusion(bf16[8,2,16,1280]{3,2,1,0:T(8,128)(2,1)S(1)} %bitcast.41, bf16[1280,1,1,1]{0,1,2,3:T(2,128)(2,1)S(1)} %reshape.68), kind=kOutput, calls=%fused_computation.7 | convolution fusion | flops 655360 | bytes 658944 | tf_op jit(solution)/shard_map/dot_general | solution.py:28
  20.8 2.8 %gather_fusion = bf16[256]{0:T(256)(128)(2,1)S(1)} fusion(bf16[2,128,4864]{2,1,0:T(8,128)(2,1)S(1)} %copy-done.1, s32[256]{0:T(256)S(1)} %fusion.18), kind=kCustom, calls=%fused_computation | custom fusion | bytes 4096 | tf_op jit(solution)/shard_map/jit(take_along_axis)/gather | solution.py:62
  23.6 5.4 %all-to-all-start.1 = ((f32[8,2,16]{2,1,0:T(2,128)}), f32[8,2,16]{2,1,0:T(2,128)S(1)}, u32[]{:S(2)}, u32[]{:S(2)}) async-start(f32[8,2,16]{2,1,0:T(2,128)} %bitcast.16), calls=%async_computation.1 | async-start | bytes 16384 | tf_op jit(solution)/shard_map/all_to_all | solution.py:32
  29.1 0.1 all_to_all.44
  29.1 6.4 %all-to-all-done.1 = f32[8,2,16]{2,1,0:T(2,128)S(1)} async-done(((f32[8,2,16]{2,1,0:T(2,128)}), f32[8,2,16]{2,1,0:T(2,128)S(1)}, u32[]{:S(2)}, u32[]{:S(2)}) %all-to-all-start.1) | async-done | bytes 1056 | tf_op jit(solution)/shard_map/all_to_all | solution.py:32
  35.5 0.1 all_to_all.47
  35.6 5.6 %all-reduce.1 = (f32[2,128]{1,0:T(2,128)S(1)}, f32[2,128]{1,0:T(2,128)S(1)}, f32[2,128]{1,0:T(2,128)S(1)}) all-reduce(f32[2,128]{1,0:T(2,128)S(1)} %and_select_fusion.1, f32[2,128]{1,0:T(2,128)S(1)} %exponential_multiply_fusion, f32[2,128]{1,0:T(2,128)S(1)} %all_to_all.47), channel_id=1, replica_groups=mesh['dp'=8,'tensor'=4] {'tensor'}, use_global_device_ids=true, to_apply=%region_6.0 | all-reduce | flops 768 | bytes 6144 | tf_op jit(solution)/shard_map/psum | solution.py:68
  41.3 0.1 multiply_multiply_fusion.1
  41.4 0.1 multiply_reduce_fusion.1
  41.5 0.3 fusion.4
  41.8 0.2 slice_reduce_fusion.1
  42.0 17.7 %all-reduce = (f32[2]{0:T(128)S(1)}, f32[2]{0:T(128)S(1)}, f32[2]{0:T(128)S(1)}) all-reduce(f32[2]{0:T(128)S(1)} %get-tuple-element.5, f32[2]{0:T(128)S(1)} %get-tuple-element.6, f32[2]{0:T(128)S(1)} %get-tuple-element.4), channel_id=1, replica_groups=mesh['dp'=8,'tensor'=4] {'dp'}, use_global_device_ids=true, to_apply=%region_5.0 | all-reduce | flops 6 | bytes 48 | tf_op jit(solution)/shard_map/psum | solution.py:49
  59.7 0.2 convolution_bitcast_fusion.1
  59.9 0.2 fusion.1
  60.1 0.1 all_to_all.48
  60.2 0.6 copy.19
  60.8 3.3 %all-to-all-start.2 = ((f32[2,8,16]{2,0,1:T(2,128)}), f32[2,8,16]{2,0,1:T(2,128)S(1)}, u32[]{:S(2)}, u32[]{:S(2)}) async-start(f32[2,8,16]{2,0,1:T(2,128)} %copy.19), calls=%async_computation.2 | async-start | bytes 16384 | tf_op jit(solution)/shard_map/all_to_all | solution.py:78
  64.1 0.6 fusion.22
  64.8 5.8 %all-to-all-done.2 = f32[2,8,16]{2,0,1:T(2,128)S(1)} async-done(((f32[2,8,16]{2,0,1:T(2,128)}), f32[2,8,16]{2,0,1:T(2,128)S(1)}, u32[]{:S(2)}, u32[]{:S(2)}) %all-to-all-start.2) | async-done | bytes 1056 | tf_op jit(solution)/shard_map/all_to_all | solution.py:78
  70.6 1.0 %multiply_convert_fusion = bf16[16,16,1280]{2,1,0:T(8,128)(2,1)} fusion(f32[1280]{0:T(1024)S(1)} %convert_element_type.29, f32[16,16]{1,0:T(8,128)S(1)} %bitcast.42), kind=kLoop, calls=%fused_computation.2 | loop fusion | flops 655360 | bytes 661504 | tf_op jit(solution)/shard_map/convert_element_type | solution.py:79
  (27 shorter events, 0.1 us)
Async XLA Ops:
  0.6 18.6 %copy-start = (bf16[16,16,1280]{2,1,0:T(8,128)(2,1)S(1)}, bf16[16,16,1280]{2,1,0:T(8,128)(2,1)}, u32[]{:S(2)}) copy-start(bf16[16,16,1280]{2,1,0:T(8,128)(2,1)} %param.20) | copy-start | bytes 1966084
  0.6 17.6 %copy-start.1 = (bf16[2,128,4864]{2,1,0:T(8,128)(2,1)S(1)}, bf16[2,128,4864]{2,1,0:T(8,128)(2,1)}, u32[]{:S(2)}) copy-start(bf16[2,128,4864]{2,1,0:T(8,128)(2,1)} %param.11) | copy-start | bytes 7471108
  2.1 21.5 %all-to-all-start = ((f32[8,2,16]{2,1,0:T(2,128)}), f32[8,2,16]{2,1,0:T(2,128)S(1)}, u32[]{:S(2)}, u32[]{:S(2)}) async-start(f32[8,2,16]{2,1,0:T(2,128)} %convert.1), calls=%async_computation | async-start | bytes 16384 | tf_op jit(solution)/shard_map/all_to_all | solution.py:33
  9.4 9.8 %copy-start.2 = (bf16[1280]{0:T(1024)(128)(2,1)S(1)}, bf16[1280]{0:T(1024)(128)(2,1)}, u32[]{:S(2)}) copy-start(bf16[1280]{0:T(1024)(128)(2,1)} %param.21) | copy-start | bytes 7684
  9.4 9.8 %copy-start.3 = (s32[2,128]{1,0:T(2,128)S(1)}, s32[2,128]{1,0:T(2,128)}, u32[]{:S(2)}) copy-start(s32[2,128]{1,0:T(2,128)} %param.12) | copy-start | bytes 3076
  11.5 29.7 %copy-start.5 = (f32[2,128]{1,0:T(2,128)S(1)}, f32[2,128]{1,0:T(2,128)}, u32[]{:S(2)}) copy-start(f32[2,128]{1,0:T(2,128)} %param.19) | copy-start | bytes 3076
  11.5 29.7 %copy-start.6 = (s32[2,128]{1,0:T(2,128)S(1)}, s32[2,128]{1,0:T(2,128)}, u32[]{:S(2)}) copy-start(s32[2,128]{1,0:T(2,128)} %param.13) | copy-start | bytes 3076
  11.5 29.7 %copy-start.8 = (s32[2]{0:T(128)S(1)}, s32[2]{0:T(128)}, u32[]{:S(2)}) copy-start(s32[2]{0:T(128)} %param.14) | copy-start | bytes 28
  11.6 29.8 %copy-start.4 = (f32[2,128]{1,0:T(2,128)S(1)}, f32[2,128]{1,0:T(2,128)}, u32[]{:S(2)}) copy-start(f32[2,128]{1,0:T(2,128)} %param.18) | copy-start | bytes 3076
  11.6 29.9 %copy-start.9 = (s32[2]{0:T(128)S(1)}, s32[2]{0:T(128)}, u32[]{:S(2)}) copy-start(s32[2]{0:T(128)} %param.15) | copy-start | bytes 28
  11.6 52.5 %copy-start.7 = (f32[2,128]{1,0:T(2,128)S(1)}, f32[2,128]{1,0:T(2,128)}, u32[]{:S(2)}) copy-start(f32[2,128]{1,0:T(2,128)} %param.16) | copy-start | bytes 3076
  23.6 12.0 %all-to-all-start.1 = ((f32[8,2,16]{2,1,0:T(2,128)}), f32[8,2,16]{2,1,0:T(2,128)S(1)}, u32[]{:S(2)}, u32[]{:S(2)}) async-start(f32[8,2,16]{2,1,0:T(2,128)} %bitcast.16), calls=%async_computation.1 | async-start | bytes 16384 | tf_op jit(solution)/shard_map/all_to_all | solution.py:32
  60.8 9.8 %all-to-all-start.2 = ((f32[2,8,16]{2,0,1:T(2,128)}), f32[2,8,16]{2,0,1:T(2,128)S(1)}, u32[]{:S(2)}, u32[]{:S(2)}) async-start(f32[2,8,16]{2,0,1:T(2,128)} %copy.19), calls=%async_computation.2 | async-start | bytes 16384 | tf_op jit(solution)/shard_map/all_to_all | solution.py:78
where the time goes:
time: 71.9 us; the launch traced here: 71.6 us
  blocking collectives  30 us (42%)
  starting transfers between devices  16 us (22%)
  waiting for transfers between devices  12.2 us (17%)
  other arithmetic  6.42 us (9%)
  local copies, waits for them, and re-layouts  3.95 us (5%)
  matrix products  2.1 us (3%)
  between operations  0.83 us (1%)
    psum x1, blocking collectives, per_device(): lax.psum((moments[0], moments[1], moments[2]), 'dp')  17.7 us
    all_to_all x1, starting transfers between devices, per_device(): lax.all_to_all(ref_logprob.astype(jnp.float32), 'dp', split_axis=0, conca...  7.28 us
    pmax x1, blocking collectives, per_device(): row_max = lax.pmax(local_top, 'tensor')  6.63 us
    all_to_all x1, waiting for transfers between devices, per_device(): lax.all_to_all(local_part, 'dp', split_axis=0, concat_axis=1, tiled=True)  6.41 us
    all_to_all x1, waiting for transfers between devices, per_device(): lax.all_to_all(grad_coeff, 'dp', split_axis=1, concat_axis=0, tiled=True)  5.8 us
    psum x1, blocking collectives, per_device(): lax.psum((rescaled, target_part, partial_value), 'tensor')  5.64 us
    all_to_all x1, starting transfers between devices, per_device(): lax.all_to_all(local_part, 'dp', split_axis=0, concat_axis=1, tiled=True)  5.43 us
    all_to_all x1, starting transfers between devices, per_device(): lax.all_to_all(grad_coeff, 'dp', split_axis=1, concat_axis=0, tiled=True)  3.33 us
  transfers between devices with their start and end apart: 3, of which 2 were waited for; matrix products, arithmetic and copies ran while one was open for 11% of the time, Pallas kernels for 0%

commit v1 on v0

--- a/solution.py
+++ b/solution.py
@@ -29,7 +29,12 @@
         all_seqs, tile_len
     )
     partial_value, ref_rows = (
-        lax.all_to_all(local_part, "dp", split_axis=0, concat_axis=1, tiled=True),
+        jnp.concatenate(
+            lax.all_to_all(
+                jnp.stack(jnp.split(local_part, lax.axis_size("dp"), axis=0)), "dp", 0, 0
+            ),
+            axis=1,
+        ),
         lax.all_to_all(
             ref_logprob.astype(jnp.float32), "dp", split_axis=0, concat_axis=1, tiled=True
         ),

time: 71.9 us -> 76 us (1.057)
  local copies, waits for them, and re-layouts: 3.95 us -> 9.25 us
  matrix products: 2.1 us -> 0.87 us
    unnamed x23 -> x30, local copies, waits for them, and re-layouts: 0.07 us -> 4.09 us
    dot_general x1, matrix products: 1.47 us -> 0.24 us  [per_device(): jnp.dot(tile_rows, value_weight, preferred_element_type=jnp.float32)]
  transfers between devices with their start and end apart: 3 -> 3, of which waited for: 2 -> 2; matrix products, arithmetic and copies ran while one was open for 11% -> 16% of each run, Pallas kernels for 0% -> 0%
where the time goes in v1:
time: 76 us; the launch traced here: 75.7 us
  blocking collectives  30 us (39%)
  starting transfers between devices  16 us (21%)
  waiting for transfers between devices  12.2 us (16%)
  local copies, waits for them, and re-layouts  9.25 us (12%)
  other arithmetic  6.41 us (8%)
  matrix products  0.87 us (1%)
  between operations  0.87 us (1%)
    psum x1, blocking collectives, per_device(): lax.psum((moments[0], moments[1], moments[2]), 'dp')  17.7 us
    all_to_all x1, starting transfers between devices, per_device(): lax.all_to_all(ref_logprob.astype(jnp.float32), 'dp', split_axis=0, conca...  7.28 us
    pmax x1, blocking collectives, per_device(): row_max = lax.pmax(local_top, 'tensor')  6.63 us
    all_to_all x1, waiting for transfers between devices, per_device(): lax.all_to_all(jnp.stack(jnp.split(local_part, lax.axis_size('dp'), axis=...  6.41 us
    all_to_all x1, waiting for transfers between devices, per_device(): lax.all_to_all(grad_coeff, 'dp', split_axis=1, concat_axis=0, tiled=True)  5.8 us
    psum x1, blocking collectives, per_device(): lax.psum((rescaled, target_part, partial_value), 'tensor')  5.64 us
    all_to_all x1, starting transfers between devices, per_device(): lax.all_to_all(jnp.stack(jnp.split(local_part, lax.axis_size('dp'), axis=...  5.43 us
    unnamed x30, local copies, waits for them, and re-layouts  4.09 us
  transfers between devices with their start and end apart: 3, of which 2 were waited for; matrix products, arithmetic and copies ran while one was open for 16% of the time, Pallas kernels for 0%

profile of v1, /device:TPU:0, one launch (start us, length us, event | category | flops | bytes accessed | tf_op | source)
XLA Modules:
  0.0 75.7 jit_solution(8027013318658561234)
XLA Ops:
  0.7 1.4 %convert.1 = f32[8,2,16]{2,1,0:T(2,128)} convert(bf16[8,2,16]{2,1,0:T(2,128)(2,1)} %bitcast.43) | non-fusion elementwise | flops 256 | bytes 1536 | tf_op jit(solution)/shard_map/all_to_all | solution.py:38
  2.1 7.3 %all-to-all-start = ((f32[8,2,16]{2,1,0:T(2,128)}), f32[8,2,16]{2,1,0:T(2,128)S(1)}, u32[]{:S(2)}, u32[]{:S(2)}) async-start(f32[8,2,16]{2,1,0:T(2,128)} %convert.1), calls=%async_computation | async-start | bytes 16384 | tf_op jit(solution)/shard_map/all_to_all | solution.py:38
  9.4 2.1 %reduce_max.9 = bf16[2,128]{1,0:T(2,128)(2,1)S(1)} reduce(bf16[2,128,4864]{2,1,0:T(8,128)(2,1)} %param.11, bf16[]{:T(256)} %constant.27.clone.1), dimensions={2}, to_apply=%region_7.0 | reduce | flops 1244928 | bytes 2490882 | tf_op jit(solution)/shard_map/reduce_max | solution.py:61
  11.6 6.6 %pmax.7 = f32[2,128]{1,0:T(2,128)S(1)} all-reduce(bf16[2,128]{1,0:T(2,128)(2,1)S(1)} %reduce_max.9), channel_id=1, replica_groups=mesh['dp'=8,'tensor'=4] {'tensor'}, use_global_device_ids=true, to_apply=%region_8.9 | all-reduce | flops 256 | bytes 1536 | tf_op jit(solution)/shard_map/pmax | solution.py:71
  18.2 1.0 %exponential_reduce_fusion = f32[2,128]{1,0:T(2,128)S(1)} fusion(bf16[2,128,4864]{2,1,0:T(8,128)(2,1)S(1)} %copy-done.1, f32[2,128]{1,0:T(2,128)S(1)} %convert_element_type.27), kind=kLoop, calls=%fused_computation.1 | loop fusion | flops 3735296 | bytes 2492416 | tf_op jit(solution)/shard_map/reduce_sum | solution.py:62
  19.3 0.2 fusion.33
  19.5 0.1 fusion.32
  20.3 0.6 constant_dynamic-update-slice_fusion.7
  20.9 0.6 constant_dynamic-update-slice_fusion.6
  21.5 0.6 constant_dynamic-update-slice_fusion.5
  22.1 0.6 constant_dynamic-update-slice_fusion.4
  22.6 0.6 constant_dynamic-update-slice_fusion.3
  23.2 0.6 constant_dynamic-update-slice_fusion.2
  23.7 0.6 constant_dynamic-update-slice_fusion.1
  24.3 0.6 constant_dynamic-update-slice_fusion
  24.9 2.8 %gather_fusion = bf16[256]{0:T(256)(128)(2,1)S(1)} fusion(bf16[2,128,4864]{2,1,0:T(8,128)(2,1)S(1)} %copy-done.1, s32[256]{0:T(256)S(1)} %fusion.16), kind=kCustom, calls=%fused_computation | custom fusion | bytes 4096 | tf_op jit(solution)/shard_map/jit(take_along_axis)/gather | solution.py:67
  27.7 5.4 %all-to-all-start.1 = ((f32[8,2,16]{2,1,0:T(2,128)}), f32[8,2,16]{2,1,0:T(2,128)S(1)}, u32[]{:S(2)}, u32[]{:S(2)}) async-start(f32[8,2,16]{2,1,0:T(2,128)} %constant_dynamic-update-slice_fusion), calls=%async_computation.1 | async-start | bytes 16384 | tf_op jit(solution)/shard_map/all_to_all | solution.py:33
  33.2 6.4 %all-to-all-done.1 = f32[8,2,16]{2,1,0:T(2,128)S(1)} async-done(((f32[8,2,16]{2,1,0:T(2,128)}), f32[8,2,16]{2,1,0:T(2,128)S(1)}, u32[]{:S(2)}, u32[]{:S(2)}) %all-to-all-start.1) | async-done | bytes 1056 | tf_op jit(solution)/shard_map/all_to_all | solution.py:33
  39.7 0.1 reshape.136
  39.7 5.6 %all-reduce.1 = (f32[2,128]{1,0:T(2,128)S(1)}, f32[2,128]{1,0:T(2,128)S(1)}, f32[2,128]{1,0:T(2,128)S(1)}) all-reduce(f32[2,128]{1,0:T(2,128)S(1)} %and_select_fusion.1, f32[2,128]{1,0:T(2,128)S(1)} %exponential_multiply_fusion, f32[2,128]{1,0:T(2,128)S(1)} %reshape.136), channel_id=1, replica_groups=mesh['dp'=8,'tensor'=4] {'tensor'}, use_global_device_ids=true, to_apply=%region_6.0 | all-reduce | flops 768 | bytes 6144 | tf_op jit(solution)/shard_map/psum | solution.py:73
  45.5 0.1 multiply_reduce_fusion.1
  45.6 0.3 fusion.2
  45.9 0.2 slice_reduce_fusion.1
  46.1 17.7 %all-reduce = (f32[2]{0:T(128)S(1)}, f32[2]{0:T(128)S(1)}, f32[2]{0:T(128)S(1)}) all-reduce(f32[2]{0:T(128)S(1)} %get-tuple-element.5, f32[2]{0:T(128)S(1)} %get-tuple-element.6, f32[2]{0:T(128)S(1)} %get-tuple-element.4), channel_id=1, replica_groups=mesh['dp'=8,'tensor'=4] {'dp'}, use_global_device_ids=true, to_apply=%region_5.0 | all-reduce | flops 6 | bytes 48 | tf_op jit(solution)/shard_map/psum | solution.py:54
  63.8 0.2 convolution_bitcast_fusion.1
  64.0 0.2 fusion.1
  64.2 0.1 all_to_all.37
  64.3 0.6 copy.22
  64.9 3.3 %all-to-all-start.2 = ((f32[2,8,16]{2,0,1:T(2,128)}), f32[2,8,16]{2,0,1:T(2,128)S(1)}, u32[]{:S(2)}, u32[]{:S(2)}) async-start(f32[2,8,16]{2,0,1:T(2,128)} %copy.22), calls=%async_computation.2 | async-start | bytes 16384 | tf_op jit(solution)/shard_map/all_to_all | solution.py:83
  68.2 0.6 fusion.20
  68.9 5.8 %all-to-all-done.2 = f32[2,8,16]{2,0,1:T(2,128)S(1)} async-done(((f32[2,8,16]{2,0,1:T(2,128)}), f32[2,8,16]{2,0,1:T(2,128)S(1)}, u32[]{:S(2)}, u32[]{:S(2)}) %all-to-all-start.2) | async-done | bytes 1056 | tf_op jit(solution)/shard_map/all_to_all | solution.py:83
  74.7 1.0 %multiply_convert_fusion = bf16[16,16,1280]{2,1,0:T(8,128)(2,1)} fusion(f32[1280]{0:T(1024)S(1)} %convert_element_type.29, f32[16,16]{1,0:T(8,128)S(1)} %bitcast.39), kind=kLoop, calls=%fused_computation.2 | loop fusion | flops 655360 | bytes 661504 | tf_op jit(solution)/shard_map/convert_element_type | solution.py:84
  (44 shorter events, 0.9 us)
Async XLA Ops:
  0.6 18.7 %copy-start = (bf16[16,16,1280]{2,1,0:T(8,128)(2,1)S(1)}, bf16[16,16,1280]{2,1,0:T(8,128)(2,1)}, u32[]{:S(2)}) copy-start(bf16[16,16,1280]{2,1,0:T(8,128)(2,1)} %param.20) | copy-start | bytes 1966084
  0.6 17.6 %copy-start.1 = (bf16[2,128,4864]{2,1,0:T(8,128)(2,1)S(1)}, bf16[2,128,4864]{2,1,0:T(8,128)(2,1)}, u32[]{:S(2)}) copy-start(bf16[2,128,4864]{2,1,0:T(8,128)(2,1)} %param.11) | copy-start | bytes 7471108
  2.1 25.6 %all-to-all-start = ((f32[8,2,16]{2,1,0:T(2,128)}), f32[8,2,16]{2,1,0:T(2,128)S(1)}, u32[]{:S(2)}, u32[]{:S(2)}) async-start(f32[8,2,16]{2,1,0:T(2,128)} %convert.1), calls=%async_computation | async-start | bytes 16384 | tf_op jit(solution)/shard_map/all_to_all | solution.py:38
  9.4 9.8 %copy-start.3 = (s32[2,128]{1,0:T(2,128)S(1)}, s32[2,128]{1,0:T(2,128)}, u32[]{:S(2)}) copy-start(s32[2,128]{1,0:T(2,128)} %param.12) | copy-start | bytes 3076
  9.4 9.9 %copy-start.2 = (bf16[1280]{0:T(1024)(128)(2,1)S(1)}, bf16[1280]{0:T(1024)(128)(2,1)}, u32[]{:S(2)}) copy-start(bf16[1280]{0:T(1024)(128)(2,1)} %param.21) | copy-start | bytes 7684
  11.5 33.9 %copy-start.5 = (f32[2,128]{1,0:T(2,128)S(1)}, f32[2,128]{1,0:T(2,128)}, u32[]{:S(2)}) copy-start(f32[2,128]{1,0:T(2,128)} %param.19) | copy-start | bytes 3076
  11.5 33.9 %copy-start.6 = (s32[2,128]{1,0:T(2,128)S(1)}, s32[2,128]{1,0:T(2,128)}, u32[]{:S(2)}) copy-start(s32[2,128]{1,0:T(2,128)} %param.13) | copy-start | bytes 3076
  11.5 33.8 %copy-start.8 = (s32[2]{0:T(128)S(1)}, s32[2]{0:T(128)}, u32[]{:S(2)}) copy-start(s32[2]{0:T(128)} %param.14) | copy-start | bytes 28
  11.6 33.9 %copy-start.4 = (f32[2,128]{1,0:T(2,128)S(1)}, f32[2,128]{1,0:T(2,128)}, u32[]{:S(2)}) copy-start(f32[2,128]{1,0:T(2,128)} %param.18) | copy-start | bytes 3076
  11.6 34.1 %copy-start.9 = (s32[2]{0:T(128)S(1)}, s32[2]{0:T(128)}, u32[]{:S(2)}) copy-start(s32[2]{0:T(128)} %param.15) | copy-start | bytes 28
  11.6 56.6 %copy-start.7 = (f32[2,128]{1,0:T(2,128)S(1)}, f32[2,128]{1,0:T(2,128)}, u32[]{:S(2)}) copy-start(f32[2,128]{1,0:T(2,128)} %param.16) | copy-start | bytes 3076
  27.7 12.0 %all-to-all-start.1 = ((f32[8,2,16]{2,1,0:T(2,128)}), f32[8,2,16]{2,1,0:T(2,128)S(1)}, u32[]{:S(2)}, u32[]{:S(2)}) async-start(f32[8,2,16]{2,1,0:T(2,128)} %constant_dynamic-update-slice_fusion), calls=%async_computation.1 | async-start | bytes 16384 | tf_op jit(solution)/shard_map/all_to_all | solution.py:33
  64.9 9.8 %all-to-all-start.2 = ((f32[2,8,16]{2,0,1:T(2,128)}), f32[2,8,16]{2,0,1:T(2,128)S(1)}, u32[]{:S(2)}, u32[]{:S(2)}) async-start(f32[2,8,16]{2,0,1:T(2,128)} %copy.22), calls=%async_computation.2 | async-start | bytes 16384 | tf_op jit(solution)/shard_map/all_to_all | solution.py:83
